TPU v7x, 256 devices: a whole 4x4x8 slice. The times are simulated.
256 devices in a mesh: mp: 64 (over y, z, core), dp: 4 (over x).
Axes of the slice: x: 4, y: 4, z: 8, core: 2. Of those that a mesh axis runs over, the one named last changes fastest.
Arguments:
- features: bfloat16 [256, 4, 4, 512], P(('dp', 'mp')), may hold values from 0 to 2
- labels: int32 [256], P('dp'), may hold values from 0 to 9
- subset_ids: int32 [64], P('mp'), may hold values from 0 to 255
- conv1_weight: bfloat16 [64, 9, 512, 512], P('mp'), may hold values from -0.09375 to 0.09375
- conv2_weight: bfloat16 [64, 9, 512, 512], P('mp'), may hold values from -0.09375 to 0.09375
- head_weight: float32 [64, 512, 10], P('mp'), may hold values from -0.25 to 0.25
Outputs:
- datamodel: float32 [256, 256], P(('dp', 'mp'))
- margin_mean: float32 [256], P(('dp', 'mp'))
- margin_norm: float32 [256], P(('dp', 'mp'))
All inputs are finite; a program needn't handle non-finite values.
Results may differ from a plain program's by a relative error of at most 0.00077.
Values may be sent and summed in bfloat16 or wider, within the bound.
A program may use at most 128 MiB of HBM per device.

v0:
```python
import functools

import jax
import jax.numpy as jnp
from jax import lax
from jax.experimental import pallas as pl
from jax.experimental.pallas import tpu as pltpu
from jax.sharding import PartitionSpec as P

SUBSETS = 256
GROUP = 8
LANES = 128
MESH = pl.DeviceIdType.MESH


def kernel(
    n, feat_ref, labels_ref, ids_ref, w1_ref, w2_ref, head_ref,
    got,
    gathered, labels, ids, w1, w2, head, lhs, msg,
    small_sem, own_sem, w1_sem, w2_sem, head_sem, fsend, frecv, msend, mrecv,
):
    me = lax.axis_index("mp")
    width = feat_ref.shape[1]
    chans = feat_ref.shape[3]
    spots = width * width
    rows = GROUP * spots
    offsets = w1_ref.shape[1]
    classes = head_ref.shape[0]

    own = pltpu.make_async_copy(feat_ref.at[0], gathered.at[me], own_sem)
    own.start()
    small_copies = [
        pltpu.make_async_copy(labels_ref, labels, small_sem.at[0]),
        pltpu.make_async_copy(ids_ref, ids, small_sem.at[1]),
    ]
    for copy in small_copies:
        copy.start()
    w1_copies = [
        pltpu.make_async_copy(w1_ref.at[0, o], w1.at[o], w1_sem.at[o]) for o in range(offsets)
    ]
    w2_copies = [
        pltpu.make_async_copy(w2_ref.at[0, o], w2.at[o], w2_sem.at[o]) for o in range(offsets)
    ]
    head_copy = pltpu.make_async_copy(head_ref, head, head_sem)

    turn = 2 * lax.div(2 * me, n) - 1
    peers = [lax.rem(me + turn * j + n, n) for j in range(1, n)]
    barrier = pltpu.get_barrier_semaphore()
    for peer in peers:
        pl.semaphore_signal(barrier, inc=1, device_id={"mp": peer}, device_id_type=MESH)
    for copy in w1_copies:
        copy.start()
    for copy in w2_copies:
        copy.start()
    head_copy.start()

    r = lax.broadcasted_iota(jnp.int32, (rows, rows), 0)
    c = lax.broadcasted_iota(jnp.int32, (rows, rows), 1)
    source = lax.rem(r, GROUP) * spots + lax.div(r, GROUP)
    reorder = jnp.where(c == source, 1.0, 0.0).astype(jnp.bfloat16)
    sub = lax.broadcasted_iota(jnp.int32, (GROUP, 1), 0)
    for copy in small_copies:
        copy.wait()
    identity = ids[0].astype(jnp.float32)
    for t in range(n):
        msg[t, 1:2, :] = jnp.full((1, LANES), identity, jnp.float32)

    own.wait()
    pl.semaphore_wait(barrier, n - 1)
    feature_sends = []
    for j, peer in enumerate(peers):
        copy = pltpu.make_async_remote_copy(
            src_ref=gathered.at[me], dst_ref=gathered.at[me],
            send_sem=fsend.at[j], recv_sem=frecv.at[me],
            device_id={"mp": peer}, device_id_type=MESH,
        )
        copy.start()
        feature_sends.append(copy)

    for copy in w1_copies:
        copy.wait()
    for copy in w2_copies:
        copy.wait()
    head_copy.wait()
    for peer in peers:
        pltpu.make_async_remote_copy(
            src_ref=gathered.at[peer], dst_ref=gathered.at[peer],
            send_sem=fsend.at[0], recv_sem=frecv.at[peer],
            device_id={"mp": peer}, device_id_type=MESH,
        ).wait_recv()

    def convolve(grid, kernel_ref):
        blank = jnp.zeros((GROUP, chans), jnp.float32)
        for o in range(offsets):
            dy, dx = o // 3 - 1, o % 3 - 1
            blocks = []
            for y in range(width):
                for x in range(width):
                    inside = 0 <= y + dy < width and 0 <= x + dx < width
                    q = ((y + dy) * width + x + dx) * GROUP
                    blocks.append(grid[q : q + GROUP] if inside else blank)
            lhs[:, o * chans : (o + 1) * chans] = jnp.concatenate(blocks, 0).astype(jnp.bfloat16)
        return jnp.dot(
            lhs[...],
            kernel_ref[...].reshape(offsets * chans, chans),
            preferred_element_type=jnp.float32,
        )

    def group(first):
        raw = gathered[pl.ds(first, GROUP)].astype(jnp.float32).reshape(rows, chans)
        grid = jnp.dot(reorder, raw.astype(jnp.bfloat16), preferred_element_type=jnp.float32)
        hidden = jnp.maximum(convolve(grid, w1), 0.0)
        block = grid + jnp.maximum(convolve(hidden, w2), 0.0)
        pooled = block[:GROUP]
        for p in range(1, spots):
            pooled = jnp.maximum(pooled, block[p * GROUP : (p + 1) * GROUP])
        label = jnp.zeros((GROUP, 1), jnp.int32)
        for t in range(GROUP):
            label = jnp.where(sub == t, labels[first + t], label)
        correct = jnp.zeros((GROUP, 1), jnp.float32)
        rival = jnp.full((GROUP, 1), -1e30, jnp.float32)
        for k in range(classes):
            logit = jnp.sum(pooled * head[k], axis=1, keepdims=True)
            correct = jnp.where(label == k, logit, correct)
            rival = jnp.where(label == k, rival, jnp.maximum(rival, logit))
        margin = jnp.broadcast_to(correct - rival, (GROUP, LANES))
        for t in range(GROUP):
            msg[first + t, 0:1, :] = margin[t : t + 1]

    if n == GROUP:
        group(0)
    else:
        pl.loop(0, n // GROUP)(lambda g: group(g * GROUP))

    margin_sends = []
    for j, peer in enumerate(peers):
        copy = pltpu.make_async_remote_copy(
            src_ref=msg.at[peer], dst_ref=got.at[me],
            send_sem=msend.at[j], recv_sem=mrecv.at[me],
            device_id={"mp": peer}, device_id_type=MESH,
        )
        copy.start()
        margin_sends.append(copy)
    got[me] = msg[me]
    for copy in feature_sends:
        copy.wait_send()
    for copy in margin_sends:
        copy.wait_send()
    for peer in peers:
        pltpu.make_async_remote_copy(
            src_ref=msg.at[peer], dst_ref=got.at[peer],
            send_sem=msend.at[0], recv_sem=mrecv.at[peer],
            device_id={"mp": peer}, device_id_type=MESH,
        ).wait_recv()


def finish(got, data_ref, mean_ref, norm_ref):
    n = got.shape[0]
    total = got[0, 0:1, :]
    for m in range(1, n):
        total = total + got[m, 0:1, :]
    mean = total / n
    spread = jnp.zeros_like(mean)
    for m in range(n):
        centred = got[m, 0:1, :] - mean
        spread = spread + centred * centred
    norm = jnp.sqrt(1.0 + spread / n)
    lane = lax.broadcasted_iota(jnp.int32, (1, LANES), 1).astype(jnp.float32)
    for start in range(0, SUBSETS, LANES):
        acc = jnp.zeros((1, LANES), jnp.float32)
        for m in range(n):
            scaled = (got[m, 0:1, :] - mean) / norm
            acc = acc + jnp.where(got[m, 1:2, :] == lane + start, scaled, 0.0)
        data_ref[:, start : start + LANES] = acc
    mean_ref[...] = mean[0, :1]
    norm_ref[...] = norm[0, :1]


def shards(n, features, labels, subset_ids, conv1_weight, conv2_weight, head_weight):
    width, chans = features.shape[1], features.shape[3]
    offsets = conv1_weight.shape[1]
    assert features.shape[0] == 1 and conv1_weight.shape[0] == 1 and n % GROUP == 0
    head = jnp.transpose(head_weight, (2, 0, 1))
    anywhere = pl.BlockSpec(memory_space=pl.ANY)
    hbm = pl.BlockSpec(memory_space=pltpu.HBM)
    vmem = pl.BlockSpec(memory_space=pltpu.VMEM)
    got = pl.pallas_call(
        functools.partial(kernel, n),
        out_shape=pltpu.VMEM((n, 2, LANES), jnp.float32),
        in_specs=[anywhere, hbm, hbm, anywhere, anywhere, anywhere],
        out_specs=vmem,
        scratch_shapes=[
            pltpu.VMEM((n, width, width, chans), features.dtype),
            pltpu.SMEM(labels.shape, labels.dtype),
            pltpu.SMEM(subset_ids.shape, subset_ids.dtype),
            pltpu.VMEM(conv1_weight.shape[1:], conv1_weight.dtype),
            pltpu.VMEM(conv2_weight.shape[1:], conv2_weight.dtype),
            pltpu.VMEM(head.shape, head.dtype),
            pltpu.VMEM((GROUP * width * width, offsets * chans), features.dtype),
            pltpu.VMEM((n, 2, LANES), jnp.float32),
            pltpu.SemaphoreType.DMA((2,)),
            pltpu.SemaphoreType.DMA,
            pltpu.SemaphoreType.DMA((offsets,)),
            pltpu.SemaphoreType.DMA((offsets,)),
            pltpu.SemaphoreType.DMA,
            pltpu.SemaphoreType.DMA((n,)),
            pltpu.SemaphoreType.DMA((n,)),
            pltpu.SemaphoreType.DMA((n,)),
            pltpu.SemaphoreType.DMA((n,)),
        ],
        compiler_params=pltpu.CompilerParams(
            collective_id=0, has_side_effects=True, vmem_limit_bytes=60 * 1024 * 1024
        ),
    )(features, labels, subset_ids, conv1_weight, conv2_weight, head)
    return pl.pallas_call(
        finish,
        out_shape=(
            jax.ShapeDtypeStruct((1, SUBSETS), jnp.float32),
            jax.ShapeDtypeStruct((1,), jnp.float32),
            jax.ShapeDtypeStruct((1,), jnp.float32),
        ),
        in_specs=[vmem],
        out_specs=(vmem, vmem, vmem),
    )(pltpu.with_memory_space_constraint(got, pltpu.VMEM))


def solution(mesh):
    in_specs = (
        P(("dp", "mp"), None, None, None),
        P("dp"),
        P("mp"),
        P("mp", None, None, None),
        P("mp", None, None, None),
        P("mp", None, None),
    )
    out_specs = (P(("dp", "mp"), None), P(("dp", "mp")), P(("dp", "mp")))
    return jax.shard_map(
        functools.partial(shards, mesh.shape["mp"]),
        mesh=mesh, in_specs=in_specs, out_specs=out_specs, check_vma=False,
    )
```

profile of v0, /device:TPU:1, one launch (start us, length us, event | category | flops | bytes accessed | tf_op | source)
XLA Modules:
  0.0 61.9 jit_solution(3127672091695871800)
XLA Ops:
  1.3 59.8 %shard_map.85.got = f32[64,2,128]{2,1,0:T(2,128)S(1)} custom-call(bf16[1,4,4,512]{3,2,1,0:T(4,128)(2,1)} %feat_ref.1, s32[64]{0:T(128)} %labels_ref.1, s32[1]{0:T(128)S(6)} %copy.9.ids_ref, bf16[1,9,512,512]{3,2,1,0:T(8,128)(2,1)} %w1_ref.1, bf16[1,9,512,512]{3,2,1,0:T(8,128)(2,1)} %w2_ref.1, f32[10,1,512]{2,1,0:T(1,128)} %bitcast.1), custom_call_target="tpu_custom_call" | custom-call | tf_op jit(solution)/shard_map/pallas_call | solution.py:187
  61.1 0.8 %shard_map.86 = (f32[1,256]{1,0:T(1,128)}, f32[1]{0:T(128)}, f32[1]{0:T(128)}) custom-call(f32[64,2,128]{2,1,0:T(2,128)S(1)} %shard_map.85.got), custom_call_target="tpu_custom_call" | custom-call | tf_op jit(solution)/shard_map/pallas_call | solution.py:215
where the time goes:
time: 62 us; the launch traced here: 61.9 us
  Pallas kernels  60.7 us (98%)
  between operations  1.28 us (2%)
    pallas_call x1, Pallas kernels, shards(): pl.pallas_call(functools.partial(kernel, n), out_shape=pltpu.VMEM((n, 2,...  59.8 us

commit v1 on v0

v1 whole, which is shorter than its diff:
```python
import functools

import jax
import jax.numpy as jnp
from jax import lax
from jax.experimental import pallas as pl
from jax.experimental.pallas import tpu as pltpu
from jax.sharding import PartitionSpec as P

SUBSETS = 256
LANES = 128
T = 16
TILE = 256
MESH = pl.DeviceIdType.MESH
NY, NZ = 4, 8

BOTH = (0, 1)
NEAR = [(0, 0), (0, 1), (0, -1), (1, 0), (-1, 0), (0, 2), (0, -2), (2, 0)]
CHUNKS = [
    [(y, z, 0) for y, z in NEAR] + [(y, z, 1) for y, z in NEAR],
    [(0, z, c) for z in (3, -3, 4) for c in BOTH]
    + [(y, z, c) for z in (1, -1) for y in (1, -1) for c in BOTH]
    + [(1, 2, 0), (-1, 2, 0)],
    [(1, 2, 1), (-1, 2, 1)]
    + [(y, z, c) for z in (-2, 3, -3) for y in (1, -1) for c in BOTH]
    + [(1, 4, 0), (-1, 4, 0)],
    [(1, 4, 1), (-1, 4, 1)] + [(2, z, c) for z in (1, -1, 2, -2, 3, -3, 4) for c in BOTH],
]


def norm(r):
    dy, dz, dc = r
    dy, dz = dy % NY, dz % NZ
    return (dy - NY if dy > NY // 2 else dy, dz - NZ if dz > NZ // 2 else dz, dc % 2)


SLOT = {norm(r): i for i, r in enumerate(sum(CHUNKS, []))}
REL = {i: r for r, i in SLOT.items()}
assert len(SLOT) == NY * NZ * 2


def minus(r, d):
    return norm((r[0] - d[0], r[1] - d[1], (r[2] + d[2]) % 2))


SIB, UP, DOWN, FAR = (0, 0, 1), (1, 0, 0), (-1, 0, 0), (2, 0, 0)
ZS = [(0, z, 0) for z in (4, 3, -3, 2, -2, 1, -1)]
PEERS = ZS + [FAR, UP, DOWN, SIB]


def kernel(
    n, feat_ref, labels_ref, ids_ref, w1_ref, w2_ref, head_ref,
    got,
    gathered, labels, ids, w1, w2, head, perm, grids, hids, msg,
    small_sem, own_sem, w1_sem, w2_sem, head_sem, fsend, frecv, msend, mrecv,
):
    me = lax.axis_index("mp")
    my = lax.div(me, 2 * NZ)
    mz = lax.rem(lax.div(me, 2), NZ)
    mc = lax.rem(me, 2)
    width = feat_ref.shape[1]
    chans = feat_ref.shape[3]
    spots = width * width
    rows = T * spots
    offsets = w1_ref.shape[1]
    classes = head_ref.shape[0]
    halves = chans // TILE

    def at(r):
        y = lax.rem(my + (r[0] % NY), NY)
        z = lax.rem(mz + (r[1] % NZ), NZ)
        c = mc if r[2] == 0 else 1 - mc
        return (y * NZ + z) * 2 + c

    own = pltpu.make_async_copy(feat_ref.at[0], gathered.at[SLOT[0, 0, 0]], own_sem)
    own.start()
    barrier = pltpu.get_barrier_semaphore()
    for r in PEERS:
        pl.semaphore_signal(barrier, inc=1, device_id={"mp": at(r)}, device_id_type=MESH)
    w1_copies = [pltpu.make_async_copy(w1_ref.at[0, o], w1.at[o], w1_sem.at[o]) for o in range(offsets)]
    w2_copies = [pltpu.make_async_copy(w2_ref.at[0, o], w2.at[o], w2_sem.at[o]) for o in range(offsets)]
    head_copy = pltpu.make_async_copy(head_ref, head, head_sem)
    small_copies = [
        pltpu.make_async_copy(labels_ref, labels, small_sem.at[0]),
        pltpu.make_async_copy(ids_ref, ids, small_sem.at[1]),
    ]
    for copy in small_copies + w1_copies + w2_copies + [head_copy]:
        copy.start()

    r_ = lax.broadcasted_iota(jnp.int32, (rows, rows), 0)
    c_ = lax.broadcasted_iota(jnp.int32, (rows, rows), 1)
    source = lax.rem(r_, T) * spots + lax.div(r_, T)
    perm[...] = jnp.where(c_ == source, 1.0, 0.0)

    sends = []

    def send(r, d):
        s = SLOT[norm(r)]
        there = SLOT[minus(r, d)]
        copy = pltpu.make_async_remote_copy(
            src_ref=gathered.at[s], dst_ref=gathered.at[there],
            send_sem=fsend.at[len(sends)], recv_sem=frecv.at[there],
            device_id={"mp": at(d)}, device_id_type=MESH,
        )
        copy.start()
        sends.append(copy)

    here = {(0, 0, 0)}

    def arrive(r):
        r = norm(r)
        if r in here:
            return
        here.add(r)
        s = SLOT[r]
        pltpu.make_async_remote_copy(
            src_ref=gathered.at[s], dst_ref=gathered.at[s],
            send_sem=fsend.at[0], recv_sem=frecv.at[s],
            device_id={"mp": at(r)}, device_id_type=MESH,
        ).wait_recv()

    def pass_on(r, *where):
        arrive(r)
        for d in where:
            send(r, d)

    def body(accs):
        def conv(stage, lhs, first, tiles):
            ring = accs[stage % len(accs)]
            for i, (rhs, pairs, depth) in enumerate(tiles):
                reg = i % 2
                for q in range(2):
                    pltpu.matmul_push_rhs(rhs(q), staging_register=reg, mxu_index=q)
                for j, (p, s) in enumerate(pairs):
                    x = lhs(s, depth)
                    for q in range(2):
                        pltpu.matmul_acc_lhs(ring[q][p], x, load_staged_rhs=reg if j == 0 else None)

        def conv_tiles(kernel_ref):
            tiles = []
            for o in range(offsets):
                dy, dx = o // 3 - 1, o % 3 - 1
                pairs = [
                    (y * width + x, (y + dy) * width + x + dx)
                    for y in range(width)
                    for x in range(width)
                    if 0 <= y + dy < width and 0 <= x + dx < width
                ]
                for k in range(halves):
                    tiles.append((
                        lambda q, o=o, k=k: kernel_ref[o, k * TILE : (k + 1) * TILE, q * TILE : (q + 1) * TILE],
                        pairs, k,
                    ))
            return tiles

        def drain(stage):
            ring = accs[stage % len(accs)]
            for p in range(spots):
                for q in range(2):
                    yield p, q, pltpu.matmul_pop(ring[q][p])

        def arrange(stage, g):
            raw = gathered[g * T : (g + 1) * T].reshape(rows, chans)
            conv(
                stage,
                lambda s, k: perm[s * T : (s + 1) * T, :],
                None,
                [(lambda q: raw[:, q * TILE : (q + 1) * TILE], [(p, p) for p in range(spots)], 0)],
            )
            for p, q, value in drain(stage):
                grids[g, p * T : (p + 1) * T, q * TILE : (q + 1) * TILE] = value

        def conv1(stage, g):
            conv(stage, lambda s, k: grids[g, s * T : (s + 1) * T, k * TILE : (k + 1) * TILE], None, conv_tiles(w1))
            for p, q, value in drain(stage):
                hids[g, p * T : (p + 1) * T, q * TILE : (q + 1) * TILE] = jnp.maximum(value, 0.0)

        def conv2(stage, g):
            conv(stage, lambda s, k: hids[g, s * T : (s + 1) * T, k * TILE : (k + 1) * TILE], None, conv_tiles(w2))
            pooled = [None] * 2
            for p, q, value in drain(stage):
                block = grids[g, p * T : (p + 1) * T, q * TILE : (q + 1) * TILE] + jnp.maximum(value, 0.0)
                pooled[q] = block if p == 0 else jnp.maximum(pooled[q], block)
            return pooled

        sub = lax.broadcasted_iota(jnp.int32, (T, 1), 0)
        lane = lax.broadcasted_iota(jnp.int32, (T, LANES), 1)

        def margins(g, pooled):
            label = jnp.zeros((T, 1), jnp.int32)
            for t in range(T):
                label = jnp.where(sub == t, labels[at(REL[g * T + t])], label)
            correct = jnp.zeros((T, 1), jnp.float32)
            rival = jnp.full((T, 1), -1e30, jnp.float32)
            for k in range(classes):
                logit = jnp.sum(
                    pooled[0] * head[k, :, :TILE] + pooled[1] * head[k, :, TILE:], axis=1, keepdims=True
                )
                correct = jnp.where(label == k, logit, correct)
                rival = jnp.where(label == k, rival, jnp.maximum(rival, logit))
            identity = ids[0].astype(jnp.float32)
            msg[g * T : (g + 1) * T, :] = jnp.where(lane < LANES // 2, correct - rival, identity)
            for t in range(T):
                s = g * T + t
                r = REL[s]
                if r == (0, 0, 0):
                    got[0:1, :] = msg[s : s + 1, :]
                    continue
                there = SLOT[minus((0, 0, 0), r)]
                copy = pltpu.make_async_remote_copy(
                    src_ref=msg.at[pl.ds(s, 1)], dst_ref=got.at[pl.ds(there, 1)],
                    send_sem=msend.at[s], recv_sem=mrecv.at[there],
                    device_id={"mp": at(r)}, device_id_type=MESH,
                )
                copy.start()
                margin_sends.append(copy)

        margin_sends = []
        for ring in accs:
            for q in range(2):
                for p in range(spots):
                    pltpu.matmul_pop(ring[q][p])
        own.wait()
        pl.semaphore_wait(barrier, len(PEERS))
        for d in PEERS:
            send((0, 0, 0), d)
        for z in (1, -1):
            pass_on((0, z, 0), UP, DOWN, SIB)
        pass_on((1, 0, 0), SIB)
        pass_on((-1, 0, 0), SIB)
        for z in (2, -2):
            pass_on((0, z, 0), UP, DOWN, SIB)
        pass_on((2, 0, 0), SIB)
        for z in (3, -3):
            pass_on((0, z, 0), UP, DOWN, SIB)

        def ready(g):
            for r in CHUNKS[g]:
                arrive(r)

        for copy in small_copies:
            copy.wait()
        ready(0)
        arrange(0, 0)
        for copy in w1_copies:
            copy.wait()
        conv1(1, 0)

        pass_on((0, 4, 0), UP, DOWN, SIB)
        for z in (1, 2):
            pass_on((1, z, 0), SIB, DOWN)
            pass_on((-1, z, 0), SIB)
        for z in (-1, -2):
            pass_on((1, z, 0), SIB)
            pass_on((-1, z, 0), SIB, UP)
        for copy in w2_copies:
            copy.wait()
        head_copy.wait()
        pooled0 = conv2(2, 0)

        pass_on((1, 3, 0), SIB, DOWN)
        pass_on((-1, 3, 0), SIB)
        pass_on((1, -3, 0), SIB)
        pass_on((-1, -3, 0), SIB, UP)
        ready(1)
        arrange(3, 1)
        margins(0, pooled0)
        conv1(4, 1)

        pass_on((1, 4, 0), SIB, DOWN)
        pass_on((-1, 4, 0), SIB)
        ready(2)
        arrange(5, 2)
        conv1(6, 2)

        for z in (1, -1, 2, -2, 3, -3):
            pass_on((2, z, 0), SIB)
        pooled1 = conv2(7, 1)

        pass_on((2, 4, 0), SIB)
        margins(1, pooled1)
        pooled2 = conv2(8, 2)

        ready(3)
        arrange(9, 3)
        margins(2, pooled2)
        conv1(10, 3)
        margins(3, conv2(11, 3))

        for copy in sends:
            copy.wait_send()
        for copy in margin_sends:
            copy.wait_send()
        for s in range(n):
            if s != SLOT[0, 0, 0]:
                pltpu.make_async_remote_copy(
                    src_ref=msg.at[pl.ds(s, 1)], dst_ref=got.at[pl.ds(s, 1)],
                    send_sem=msend.at[0], recv_sem=mrecv.at[s],
                    device_id={"mp": at(REL[s])}, device_id_type=MESH,
                ).wait_recv()

    acc = lambda q: pltpu.ACC(q)((T, TILE), jnp.float32)
    pl.run_scoped(body, tuple(tuple(tuple(acc(q) for _ in range(spots)) for q in range(2)) for _ in range(4)))


def finish(got, data_ref, mean_ref, norm_ref):
    n = got.shape[0]
    half = LANES // 2
    lane = lax.broadcasted_iota(jnp.int32, (n, LANES), 1)
    both = got[...]
    swapped = pltpu.roll(both, half, 1)
    margin = jnp.where(lane < half, both, swapped)
    identity = jnp.where(lane < half, swapped, both)
    mean = jnp.sum(margin, axis=0, keepdims=True) / n
    centred = margin - mean
    norm_ = jnp.sqrt(1.0 + jnp.sum(centred * centred, axis=0, keepdims=True) / n)
    scaled = centred / norm_
    for start in range(0, SUBSETS, LANES):
        here = identity == (lane + start).astype(jnp.float32)
        data_ref[:, start : start + LANES] = jnp.sum(jnp.where(here, scaled, 0.0), axis=0, keepdims=True)
    mean_ref[...] = mean[0, :1]
    norm_ref[...] = norm_[0, :1]


def shards(n, features, labels, subset_ids, conv1_weight, conv2_weight, head_weight):
    width, chans = features.shape[1], features.shape[3]
    offsets = conv1_weight.shape[1]
    spots = width * width
    assert features.shape[0] == 1 and conv1_weight.shape[0] == 1 and n == NY * NZ * 2
    features = features.reshape(1, spots, chans) if False else features
    head = jnp.transpose(head_weight, (2, 0, 1))
    anywhere = pl.BlockSpec(memory_space=pl.ANY)
    hbm = pl.BlockSpec(memory_space=pltpu.HBM)
    vmem = pl.BlockSpec(memory_space=pltpu.VMEM)
    chunks = n // T
    got = pl.pallas_call(
        functools.partial(kernel, n),
        out_shape=pltpu.VMEM((n, LANES), jnp.float32),
        in_specs=[anywhere, hbm, hbm, anywhere, anywhere, anywhere],
        out_specs=vmem,
        scratch_shapes=[
            pltpu.VMEM((n, width, width, chans), features.dtype),
            pltpu.SMEM(labels.shape, labels.dtype),
            pltpu.SMEM(subset_ids.shape, subset_ids.dtype),
            pltpu.VMEM(conv1_weight.shape[1:], conv1_weight.dtype),
            pltpu.VMEM(conv2_weight.shape[1:], conv2_weight.dtype),
            pltpu.VMEM(head.shape, head.dtype),
            pltpu.VMEM((T * spots, T * spots), jnp.float32),
            pltpu.VMEM((chunks, T * spots, chans), jnp.float32),
            pltpu.VMEM((chunks, T * spots, chans), jnp.float32),
            pltpu.VMEM((n, LANES), jnp.float32),
            pltpu.SemaphoreType.DMA((2,)),
            pltpu.SemaphoreType.DMA,
            pltpu.SemaphoreType.DMA((offsets,)),
            pltpu.SemaphoreType.DMA((offsets,)),
            pltpu.SemaphoreType.DMA,
            pltpu.SemaphoreType.DMA((80,)),
            pltpu.SemaphoreType.DMA((n,)),
            pltpu.SemaphoreType.DMA((n,)),
            pltpu.SemaphoreType.DMA((n,)),
        ],
        compiler_params=pltpu.CompilerParams(
            collective_id=0, has_side_effects=True, vmem_limit_bytes=60 * 1024 * 1024
        ),
    )(features, labels, subset_ids, conv1_weight, conv2_weight, head)
    return pl.pallas_call(
        finish,
        out_shape=(
            jax.ShapeDtypeStruct((1, SUBSETS), jnp.float32),
            jax.ShapeDtypeStruct((1,), jnp.float32),
            jax.ShapeDtypeStruct((1,), jnp.float32),
        ),
        in_specs=[vmem],
        out_specs=(vmem, vmem, vmem),
    )(pltpu.with_memory_space_constraint(got, pltpu.VMEM))


def solution(mesh):
    in_specs = (
        P(("dp", "mp"), None, None, None),
        P("dp"),
        P("mp"),
        P("mp", None, None, None),
        P("mp", None, None, None),
        P("mp", None, None),
    )
    out_specs = (P(("dp", "mp"), None), P(("dp", "mp")), P(("dp", "mp")))
    return jax.shard_map(
        functools.partial(shards, mesh.shape["mp"]),
        mesh=mesh, in_specs=in_specs, out_specs=out_specs, check_vma=False,
    )
```

time: 62 us -> 37.6 us (0.61)
  Pallas kernels: 60.7 us -> 36.1 us
    pallas_call x1, Pallas kernels: 59.8 us -> 35.4 us  [shards(): pl.pallas_call(functools.partial(kernel, n), out_shape=pltpu.VMEM((n, LAN...]
where the time goes in v1:
time: 37.6 us; the launch traced here: 37.4 us
  Pallas kernels  36.1 us (96%)
  between operations  1.28 us (3%)
    pallas_call x1, Pallas kernels, shards(): pl.pallas_call(functools.partial(kernel, n), out_shape=pltpu.VMEM((n, LAN...  35.4 us

profile of v1, /device:TPU:1, one launch (start us, length us, event | category | flops | bytes accessed | tf_op | source)
XLA Modules:
  0.0 37.4 jit_solution(5942032431182435708)
XLA Ops:
  1.3 35.4 %shard_map.85.got = f32[64,128]{1,0:T(8,128)S(1)} custom-call(bf16[1,4,4,512]{3,2,1,0:T(4,128)(2,1)} %feat_ref.1, s32[64]{0:T(128)} %labels_ref.1, s32[1]{0:T(128)S(6)} %copy.9.ids_ref, bf16[1,9,512,512]{3,2,1,0:T(8,128)(2,1)} %w1_ref.1, bf16[1,9,512,512]{3,2,1,0:T(8,128)(2,1)} %w2_ref.1, f32[10,1,512]{2,1,0:T(1,128)} %bitcast.1), custom_call_target="tpu_custom_call" | custom-call | tf_op jit(solution)/shard_map/pallas_call | solution.py:336
  36.7 0.7 %shard_map.86 = (f32[1,256]{1,0:T(1,128)}, f32[1]{0:T(128)}, f32[1]{0:T(128)}) custom-call(f32[64,128]{1,0:T(8,128)S(1)} %shard_map.85.got), custom_call_target="tpu_custom_call" | custom-call | tf_op jit(solution)/shard_map/pallas_call | solution.py:366

commit v2 on v1

v2 whole, which is shorter than its diff:
```python
import functools

import jax
import jax.numpy as jnp
from jax import lax
from jax.experimental import pallas as pl
from jax.experimental.pallas import tpu as pltpu
from jax.sharding import PartitionSpec as P

SUBSETS = 256
LANES = 128
TILE = 256
MESH = pl.DeviceIdType.MESH
NY, NZ = 4, 8
BOTH = (1, -1)

CHUNKS = [
    [(y, z, c) for c in (0, 1) for y, z in ((0, 0), (0, 1), (0, -1), (1, 0), (-1, 0), (0, 2), (0, -2), (2, 0))],
    [(y, z, 0) for y in BOTH for z in BOTH]
    + [(2, 1, 0), (2, -1, 0)]
    + [(y, 2 * z, 0) for y in BOTH for z in BOTH]
    + [(y, z, 1) for y in BOTH for z in BOTH]
    + [(2, 1, 1), (2, -1, 1)],
    [(2, 2, 0), (2, -2, 0), (0, 3, 0), (0, -3, 0), (0, 4, 0), (1, 3, 0), (-1, 3, 0)]
    + [(y, 2 * z, 1) for y in BOTH for z in BOTH]
    + [(2, 2, 1), (2, -2, 1), (0, 3, 1), (0, -3, 1), (0, 4, 1)],
    [(y, z, 0) for y, z in ((1, -3), (-1, -3), (2, 3), (2, -3), (1, 4), (-1, 4), (2, 4))]
    + [(y, z, 1) for y, z in ((1, -3), (-1, -3), (2, 3), (2, -3), (1, 4), (-1, 4), (2, 4), (1, 3), (-1, 3))],
]
STARTS = [sum(map(len, CHUNKS[:g])) for g in range(len(CHUNKS))]


def norm(r):
    dy, dz, dc = r
    dy, dz = dy % NY, dz % NZ
    return (dy - NY if dy > NY // 2 else dy, dz - NZ if dz > NZ // 2 else dz, dc % 2)


REL = sum(CHUNKS, [])
SLOT = {norm(r): i for i, r in enumerate(REL)}
CHUNK_OF = {norm(r): g for g, chunk in enumerate(CHUNKS) for r in chunk}
assert len(SLOT) == len(REL) == NY * NZ * 2


def minus(r, d):
    return norm((r[0] - d[0], r[1] - d[1], (r[2] + d[2]) % 2))


SIB, UP, DOWN, FAR = (0, 0, 1), (1, 0, 0), (-1, 0, 0), (2, 0, 0)
COLUMN = [FAR, UP, DOWN]
NEXT = [SIB, (0, 1, 0), (0, -1, 0), UP, DOWN, (0, 2, 0), (0, -2, 0), FAR]
SENDS = 63


def kernel(
    n, feat_ref, labels_ref, ids_ref, w1_ref, w2_ref, head_ref,
    got,
    gathered, labels, ids, w1, w2, head, grids, hids, msg,
    mid, small_sem, own_sem, w1_sem, w2_sem, head_sem, fsend, frecv, grecv, msend, mrecv,
):
    me = lax.axis_index("mp")
    my = lax.div(me, 2 * NZ)
    mz = lax.rem(lax.div(me, 2), NZ)
    mc = lax.rem(me, 2)
    width = feat_ref.shape[1]
    chans = feat_ref.shape[3]
    spots = width * width
    offsets = w1_ref.shape[1]
    classes = head_ref.shape[0]
    halves = chans // TILE

    def at(r):
        y = lax.rem(my + (r[0] % NY), NY)
        z = lax.rem(mz + (r[1] % NZ), NZ)
        c = mc if r[2] == 0 else 1 - mc
        return (y * NZ + z) * 2 + c

    own = pltpu.make_async_copy(feat_ref.at[0], gathered.at[0], own_sem)
    own.start()
    barrier = pltpu.get_barrier_semaphore()
    for r in NEXT:
        pl.semaphore_signal(barrier, inc=1, device_id={"mp": at(r)}, device_id_type=MESH)
    small_copies = [
        pltpu.make_async_copy(labels_ref, labels, small_sem.at[0]),
        pltpu.make_async_copy(ids_ref, ids, small_sem.at[1]),
    ]
    for copy in small_copies:
        copy.start()
    for o in range(offsets):
        pltpu.make_async_copy(w1_ref.at[0, o], w1.at[o], w1_sem).start()
    for o in range(offsets):
        pltpu.make_async_copy(w2_ref.at[0, o], w2.at[o], w2_sem).start()
    head_copy = pltpu.make_async_copy(head_ref, head, head_sem)
    head_copy.start()

    sent = []

    def send(r, d):
        s = SLOT[norm(r)]
        source = minus(r, d)
        there = SLOT[source]
        pltpu.make_async_remote_copy(
            src_ref=gathered.at[s], dst_ref=gathered.at[there],
            send_sem=fsend, recv_sem=grecv.at[CHUNK_OF[source]] if source[2] else frecv.at[there],
            device_id={"mp": at(d)}, device_id_type=MESH,
        ).start()
        sent.append(d)

    here = {(0, 0, 0)}

    def arrive(r):
        r = norm(r)
        if r in here:
            return
        here.add(r)
        s = SLOT[r]
        pltpu.make_async_copy(gathered.at[s], gathered.at[s], frecv.at[s]).wait()

    def pass_on(r, *where):
        arrive(r)
        for d in where:
            send(r, d)

    def ready(g):
        others = [r for r in CHUNKS[g] if r[2]]
        for r in CHUNKS[g]:
            if not r[2]:
                arrive(r)
        block = gathered.at[pl.ds(SLOT[norm(others[0])], len(others))]
        pltpu.make_async_copy(block, block, grecv.at[g]).wait()

    def body(rings):
        turns = []

        def take(t):
            turns.append(t)
            return rings[(len(turns) - 1) % len(rings)]

        def multiply(ring, lhs, tiles, between={}):
            for i, (rhs, pairs, depth) in enumerate(tiles):
                reg = i % 2
                for q in range(2):
                    pltpu.matmul_push_rhs(rhs(q), staging_register=reg, mxu_index=q)
                for j, (p, s) in enumerate(pairs):
                    x = lhs(s, depth)
                    for q in range(2):
                        pltpu.matmul_acc_lhs(ring[q][p], x, load_staged_rhs=reg if j == 0 else None)
                if i in between:
                    between[i]()

        def conv_tiles(kernel_ref):
            tiles = []
            for o in range(offsets):
                dy, dx = o // 3 - 1, o % 3 - 1
                pairs = [
                    (y * width + x, (y + dy) * width + x + dx)
                    for y in range(width)
                    for x in range(width)
                    if 0 <= y + dy < width and 0 <= x + dx < width
                ]
                for k in range(halves):
                    tiles.append((
                        lambda q, o=o, k=k: kernel_ref[o, k * TILE : (k + 1) * TILE, q * TILE : (q + 1) * TILE],
                        pairs, k,
                    ))
            return tiles

        def drain(ring):
            for p in range(spots):
                for q in range(2):
                    yield p, q, pltpu.matmul_pop(ring[q][p])

        def place(g, p, k):
            t = len(CHUNKS[g])
            first = STARTS[g] * spots + p * t
            return (slice(first, first + t), slice(k * TILE, (k + 1) * TILE))

        def arrange(g):
            t = len(CHUNKS[g])
            ring = take(t)
            raw = gathered[STARTS[g] : STARTS[g] + t].reshape(t * spots, chans)
            if t * spots < TILE:
                raw = jnp.concatenate([raw, jnp.zeros((TILE - t * spots, chans), raw.dtype)], 0)
            row = lax.broadcasted_iota(jnp.int32, (t, TILE), 0)
            col = lax.broadcasted_iota(jnp.int32, (t, TILE), 1)
            multiply(
                ring,
                lambda s, k: jnp.where(col == row * spots + s, 1.0, 0.0),
                [(lambda q: raw[:, q * TILE : (q + 1) * TILE], [(p, p) for p in range(spots)], 0)],
            )
            return ring

        def arranged(g, ring):
            for p, q, value in drain(ring):
                grids[place(g, p, q)] = value

        def conv1(g, between={}):
            ring = take(len(CHUNKS[g]))
            multiply(ring, lambda s, k: grids[place(g, s, k)], conv_tiles(w1), between)
            return ring

        def conv1d(g, ring):
            for p, q, value in drain(ring):
                hids[place(g, p, q)] = jnp.maximum(value, 0.0)

        def conv2(g, between={}):
            ring = take(len(CHUNKS[g]))
            multiply(ring, lambda s, k: hids[place(g, s, k)], conv_tiles(w2), between)
            return ring

        def conv2d(g, ring):
            pooled = [None] * 2
            for p, q, value in drain(ring):
                block = grids[place(g, p, q)] + jnp.maximum(value, 0.0)
                pooled[q] = block if p == 0 else jnp.maximum(pooled[q], block)
            return pooled

        def margins(g, pooled):
            t = len(CHUNKS[g])
            sub = lax.broadcasted_iota(jnp.int32, (t, 1), 0)
            lane = lax.broadcasted_iota(jnp.int32, (t, LANES), 1)
            label = jnp.zeros((t, 1), jnp.int32)
            for i, r in enumerate(CHUNKS[g]):
                label = jnp.where(sub == i, labels[at(r)], label)
            correct = jnp.zeros((t, 1), jnp.float32)
            rival = jnp.full((t, 1), -1e30, jnp.float32)
            for k in range(classes):
                logit = jnp.sum(
                    pooled[0] * head[k, :, :TILE] + pooled[1] * head[k, :, TILE:], axis=1, keepdims=True
                )
                correct = jnp.where(label == k, logit, correct)
                rival = jnp.where(label == k, rival, jnp.maximum(rival, logit))
            identity = ids[0].astype(jnp.float32)
            first = STARTS[g]
            msg[first : first + t, :] = jnp.where(lane < LANES // 2, correct - rival, identity)
            for i, r in enumerate(CHUNKS[g]):
                s = first + i
                if r == (0, 0, 0):
                    got[0:1, :] = msg[0:1, :]
                    continue
                there = SLOT[minus((0, 0, 0), r)]
                pltpu.make_async_remote_copy(
                    src_ref=msg.at[pl.ds(s, 1)], dst_ref=got.at[pl.ds(there, 1)],
                    send_sem=msend, recv_sem=mrecv,
                    device_id={"mp": at(r)}, device_id_type=MESH,
                ).start()

        for ring in rings:
            for q in range(2):
                for p in range(spots):
                    pltpu.matmul_pop(ring[q][p])
        pl.semaphore_wait(barrier, len(NEXT))
        for i, z in enumerate((2, -2)):
            pl.semaphore_signal(mid.at[i], inc=1, device_id={"mp": at((0, z, 0))}, device_id_type=MESH)
        own.wait()
        for d in NEXT:
            send((0, 0, 0), d)
        for i in range(2):
            pl.semaphore_wait(mid.at[i], 1)
        for z in (3, -3, 4):
            send((0, 0, 0), (0, z, 0))
        for z in BOTH:
            pass_on((0, z, 0), SIB, *COLUMN)
        for y in BOTH:
            pass_on((y, 0, 0), SIB)
        for z in BOTH:
            pass_on((0, 2 * z, 0), SIB, *COLUMN)
        pass_on((2, 0, 0), SIB)
        for copy in small_copies:
            copy.wait()
        pltpu.make_async_copy(w1, w1, w1_sem).wait()
        pltpu.make_async_copy(w2, w2, w2_sem).wait()
        head_copy.wait()
        ready(0)
        arranged(0, arrange(0))

        def ones():
            for y in BOTH:
                for z in BOTH:
                    pass_on((y, z, 0), SIB)

        def threes():
            for z in BOTH:
                pass_on((0, 3 * z, 0), *COLUMN, SIB)
            for z in BOTH:
                pass_on((2, z, 0), SIB)

        def four():
            pass_on((0, 4, 0), *COLUMN, *[(y, 0, 1) for y, _, _ in COLUMN], SIB)
            for z in BOTH:
                pass_on((2, 2 * z, 0), SIB)

        first = conv1(0, {5: ones, 11: threes})
        for y in BOTH:
            for z in BOTH:
                pass_on((y, 2 * z, 0), SIB)
        conv1d(0, first)
        second = conv2(0, {11: four})
        ready(1)
        arrange1 = arrange(1)
        pooled0 = conv2d(0, second)
        arranged(1, arrange1)

        def last():
            for y in BOTH:
                for z in BOTH:
                    pass_on((y, 3 * z, 0), SIB)
            for z in BOTH:
                pass_on((2, 3 * z, 0), SIB)

        first1 = conv1(1, {15: last})
        margins(0, pooled0)
        ready(2)
        arrange2 = arrange(2)
        conv1d(1, first1)
        arranged(2, arrange2)
        first2 = conv1(2)
        second1 = conv2(1)
        conv1d(2, first2)
        ready(3)
        arrange3 = arrange(3)
        pooled1 = conv2d(1, second1)
        arranged(3, arrange3)
        first3 = conv1(3)
        margins(1, pooled1)
        second2 = conv2(2)
        conv1d(3, first3)
        pooled2 = conv2d(2, second2)
        second3 = conv2(3)
        margins(2, pooled2)
        margins(3, conv2d(3, second3))

        assert len(sent) == SENDS
        pltpu.make_async_copy(gathered.at[pl.ds(0, SENDS)], gathered.at[pl.ds(0, SENDS)], fsend).wait()
        pltpu.make_async_copy(msg.at[pl.ds(1, n - 1)], msg.at[pl.ds(1, n - 1)], msend).wait()
        pltpu.make_async_copy(got.at[pl.ds(1, n - 1)], got.at[pl.ds(1, n - 1)], mrecv).wait()

    def rings(count, t):
        return tuple(
            tuple(tuple(pltpu.ACC(q)((t, TILE), jnp.float32) for _ in range(spots)) for q in range(2))
            for _ in range(count)
        )

    pl.run_scoped(body, rings(4, 16))


def finish(got, data_ref, mean_ref, norm_ref):
    n = got.shape[0]
    half = LANES // 2
    lane = lax.broadcasted_iota(jnp.int32, (n, LANES), 1)
    both = got[...]
    swapped = pltpu.roll(both, half, 1)
    margin = jnp.where(lane < half, both, swapped)
    identity = jnp.where(lane < half, swapped, both)
    mean = jnp.sum(margin, axis=0, keepdims=True) / n
    centred = margin - mean
    norm_ = jnp.sqrt(1.0 + jnp.sum(centred * centred, axis=0, keepdims=True) / n)
    scaled = centred / norm_
    for start in range(0, SUBSETS, LANES):
        here = identity == (lane + start).astype(jnp.float32)
        data_ref[:, start : start + LANES] = jnp.sum(jnp.where(here, scaled, 0.0), axis=0, keepdims=True)
    mean_ref[...] = mean[0, :1]
    norm_ref[...] = norm_[0, :1]


def shards(n, features, labels, subset_ids, conv1_weight, conv2_weight, head_weight):
    width, chans = features.shape[1], features.shape[3]
    offsets = conv1_weight.shape[1]
    spots = width * width
    assert features.shape[0] == 1 and conv1_weight.shape[0] == 1 and n == NY * NZ * 2
    head = jnp.transpose(head_weight, (2, 0, 1))
    anywhere = pl.BlockSpec(memory_space=pl.ANY)
    hbm = pl.BlockSpec(memory_space=pltpu.HBM)
    vmem = pl.BlockSpec(memory_space=pltpu.VMEM)
    got = pl.pallas_call(
        functools.partial(kernel, n),
        out_shape=pltpu.VMEM((n, LANES), jnp.float32),
        in_specs=[anywhere, hbm, hbm, anywhere, anywhere, anywhere],
        out_specs=vmem,
        scratch_shapes=[
            pltpu.VMEM((n, width, width, chans), features.dtype),
            pltpu.SMEM(labels.shape, labels.dtype),
            pltpu.SMEM(subset_ids.shape, subset_ids.dtype),
            pltpu.VMEM(conv1_weight.shape[1:], conv1_weight.dtype),
            pltpu.VMEM(conv2_weight.shape[1:], conv2_weight.dtype),
            pltpu.VMEM(head.shape, head.dtype),
            pltpu.VMEM((n * spots, chans), jnp.float32),
            pltpu.VMEM((n * spots, chans), jnp.float32),
            pltpu.VMEM((n, LANES), jnp.float32),
            pltpu.SemaphoreType.REGULAR((2,)),
            pltpu.SemaphoreType.DMA((2,)),
            pltpu.SemaphoreType.DMA,
            pltpu.SemaphoreType.DMA,
            pltpu.SemaphoreType.DMA,
            pltpu.SemaphoreType.DMA,
            pltpu.SemaphoreType.DMA,
            pltpu.SemaphoreType.DMA((n,)),
            pltpu.SemaphoreType.DMA((len(CHUNKS),)),
            pltpu.SemaphoreType.DMA,
            pltpu.SemaphoreType.DMA,
        ],
        compiler_params=pltpu.CompilerParams(
            collective_id=0, has_side_effects=True, vmem_limit_bytes=60 * 1024 * 1024
        ),
    )(features, labels, subset_ids, conv1_weight, conv2_weight, head)
    return pl.pallas_call(
        finish,
        out_shape=(
            jax.ShapeDtypeStruct((1, SUBSETS), jnp.float32),
            jax.ShapeDtypeStruct((1,), jnp.float32),
            jax.ShapeDtypeStruct((1,), jnp.float32),
        ),
        in_specs=[vmem],
        out_specs=(vmem, vmem, vmem),
    )(pltpu.with_memory_space_constraint(got, pltpu.VMEM))


def solution(mesh):
    in_specs = (
        P(("dp", "mp"), None, None, None),
        P("dp"),
        P("mp"),
        P("mp", None, None, None),
        P("mp", None, None, None),
        P("mp", None, None),
    )
    out_specs = (P(("dp", "mp"), None), P(("dp", "mp")), P(("dp", "mp")))
    return jax.shard_map(
        functools.partial(shards, mesh.shape["mp"]),
        mesh=mesh, in_specs=in_specs, out_specs=out_specs, check_vma=False,
    )
```

time: 37.6 us -> 33.6 us (0.89)
  Pallas kernels: 36.1 us -> 32.3 us
    pallas_call x1, Pallas kernels: 35.4 us -> 31.6 us  [shards(): pl.pallas_call(functools.partial(kernel, n), out_shape=pltpu.VMEM((n, LAN...]
where the time goes in v2:
time: 33.6 us
  Pallas kernels  32.3 us (96%)
  between operations  1.28 us (4%)
    pallas_call x1, Pallas kernels, shards(): pl.pallas_call(functools.partial(kernel, n), out_shape=pltpu.VMEM((n, LAN...  31.6 us
    pallas_call x1, Pallas kernels, shards(): pl.pallas_call(finish, out_shape=(jax.ShapeDtypeStruct((1, SUBSETS), jnp....  0.7 us

profile of v2, /device:TPU:1, one launch (start us, length us, event | category | flops | bytes accessed | tf_op | source)
XLA Modules:
  0.0 33.6 jit_solution(1589697569094752843)
XLA Ops:
  1.3 31.6 %shard_map.85.got = f32[64,128]{1,0:T(8,128)S(1)} custom-call(bf16[1,4,4,512]{3,2,1,0:T(4,128)(2,1)} %feat_ref.1, s32[64]{0:T(128)} %labels_ref.1, s32[1]{0:T(128)S(6)} %copy.9.ids_ref, bf16[1,9,512,512]{3,2,1,0:T(8,128)(2,1)} %w1_ref.1, bf16[1,9,512,512]{3,2,1,0:T(8,128)(2,1)} %w2_ref.1, f32[10,1,512]{2,1,0:T(1,128)} %bitcast.1), custom_call_target="tpu_custom_call" | custom-call | tf_op jit(solution)/shard_map/pallas_call | solution.py:375
  32.9 0.7 %shard_map.86 = (f32[1,256]{1,0:T(1,128)}, f32[1]{0:T(128)}, f32[1]{0:T(128)}) custom-call(f32[64,128]{1,0:T(8,128)S(1)} %shard_map.85.got), custom_call_target="tpu_custom_call" | custom-call | tf_op jit(solution)/shard_map/pallas_call | solution.py:406

commit v3 on v2

--- a/solution.py
+++ b/solution.py
@@ -19,11 +19,11 @@
     [(y, z, 0) for y in BOTH for z in BOTH]
     + [(2, 1, 0), (2, -1, 0)]
     + [(y, 2 * z, 0) for y in BOTH for z in BOTH]
-    + [(y, z, 1) for y in BOTH for z in BOTH]
-    + [(2, 1, 1), (2, -1, 1)],
-    [(2, 2, 0), (2, -2, 0), (0, 3, 0), (0, -3, 0), (0, 4, 0), (1, 3, 0), (-1, 3, 0)]
+    + [(0, 3, 0), (0, -3, 0)]
+    + [(y, z, 1) for y in BOTH for z in BOTH],
+    [(2, 2, 0), (2, -2, 0), (0, 4, 0), (1, 3, 0), (-1, 3, 0), (0, 3, 1), (0, -3, 1), (2, 1, 1), (2, -1, 1)]
     + [(y, 2 * z, 1) for y in BOTH for z in BOTH]
-    + [(2, 2, 1), (2, -2, 1), (0, 3, 1), (0, -3, 1), (0, 4, 1)],
+    + [(2, 2, 1), (2, -2, 1), (0, 4, 1)],
     [(y, z, 0) for y, z in ((1, -3), (-1, -3), (2, 3), (2, -3), (1, 4), (-1, 4), (2, 4))]
     + [(y, z, 1) for y, z in ((1, -3), (-1, -3), (2, 3), (2, -3), (1, 4), (-1, 4), (2, 4), (1, 3), (-1, 3))],
 ]
@@ -177,41 +177,35 @@
 
         def arrange(g):
             t = len(CHUNKS[g])
-            ring = take(t)
-            raw = gathered[STARTS[g] : STARTS[g] + t].reshape(t * spots, chans)
-            if t * spots < TILE:
-                raw = jnp.concatenate([raw, jnp.zeros((TILE - t * spots, chans), raw.dtype)], 0)
-            row = lax.broadcasted_iota(jnp.int32, (t, TILE), 0)
-            col = lax.broadcasted_iota(jnp.int32, (t, TILE), 1)
-            multiply(
-                ring,
-                lambda s, k: jnp.where(col == row * spots + s, 1.0, 0.0),
-                [(lambda q: raw[:, q * TILE : (q + 1) * TILE], [(p, p) for p in range(spots)], 0)],
-            )
-            return ring
-
-        def arranged(g, ring):
-            for p, q, value in drain(ring):
-                grids[place(g, p, q)] = value
+            for i in range(t):
+                for y in range(width):
+                    first = STARTS[g] * spots + y * width * t + i
+                    line = gathered[STARTS[g] + i, y].astype(jnp.float32)
+                    for c in range(chans // LANES):
+                        grids[c, pl.ds(first, width, stride=t), :] = line[:, c * LANES : (c + 1) * LANES]
+
+        def grid(g, p, k):
+            rows = place(g, p, k)[0]
+            return jnp.concatenate([grids[c, rows, :] for c in range(k * TILE // LANES, (k + 1) * TILE // LANES)], 1)
 
         def conv1(g, between={}):
             ring = take(len(CHUNKS[g]))
-            multiply(ring, lambda s, k: grids[place(g, s, k)], conv_tiles(w1), between)
+            multiply(ring, lambda s, k: grid(g, s, k), conv_tiles(w1), between)
             return ring
 
         def conv1d(g, ring):
             for p, q, value in drain(ring):
                 hids[place(g, p, q)] = jnp.maximum(value, 0.0)
 
-        def conv2(g, between={}):
-            ring = take(len(CHUNKS[g]))
-            multiply(ring, lambda s, k: hids[place(g, s, k)], conv_tiles(w2), between)
+        def conv2(g, between={}, ring=None, part=slice(None)):
+            ring = ring or take(len(CHUNKS[g]))
+            multiply(ring, lambda s, k: hids[place(g, s, k)], conv_tiles(w2)[part], between)
             return ring
 
         def conv2d(g, ring):
             pooled = [None] * 2
             for p, q, value in drain(ring):
-                block = grids[place(g, p, q)] + jnp.maximum(value, 0.0)
+                block = grid(g, p, q) + jnp.maximum(value, 0.0)
                 pooled[q] = block if p == 0 else jnp.maximum(pooled[q], block)
             return pooled
 
@@ -233,6 +227,9 @@
             identity = ids[0].astype(jnp.float32)
             first = STARTS[g]
             msg[first : first + t, :] = jnp.where(lane < LANES // 2, correct - rival, identity)
+
+        def tell(g):
+            first = STARTS[g]
             for i, r in enumerate(CHUNKS[g]):
                 s = first + i
                 if r == (0, 0, 0):
@@ -272,63 +269,63 @@
         pltpu.make_async_copy(w2, w2, w2_sem).wait()
         head_copy.wait()
         ready(0)
-        arranged(0, arrange(0))
-
-        def ones():
+        arrange(0)
+
+        def four():
+            for z in BOTH:
+                pass_on((2, z, 0), SIB)
+            pass_on((0, 4, 0), *COLUMN, *[(y, 0, 1) for y, _, _ in COLUMN], SIB)
+
+        def two_off():
             for y in BOTH:
                 for z in BOTH:
-                    pass_on((y, z, 0), SIB)
-
-        def threes():
-            for z in BOTH:
-                pass_on((0, 3 * z, 0), *COLUMN, SIB)
-            for z in BOTH:
-                pass_on((2, z, 0), SIB)
-
-        def four():
-            pass_on((0, 4, 0), *COLUMN, *[(y, 0, 1) for y, _, _ in COLUMN], SIB)
+                    pass_on((y, 2 * z, 0), SIB)
             for z in BOTH:
                 pass_on((2, 2 * z, 0), SIB)
 
-        first = conv1(0, {5: ones, 11: threes})
-        for y in BOTH:
-            for z in BOTH:
-                pass_on((y, 2 * z, 0), SIB)
-        conv1d(0, first)
-        second = conv2(0, {11: four})
-        ready(1)
-        arrange1 = arrange(1)
-        pooled0 = conv2d(0, second)
-        arranged(1, arrange1)
-
-        def last():
+        def three_off():
             for y in BOTH:
                 for z in BOTH:
                     pass_on((y, 3 * z, 0), SIB)
             for z in BOTH:
                 pass_on((2, 3 * z, 0), SIB)
 
-        first1 = conv1(1, {15: last})
+        first0 = conv1(0)
+        for z in BOTH:
+            pass_on((0, 3 * z, 0), *COLUMN, SIB)
+        for y in BOTH:
+            for z in BOTH:
+                pass_on((y, z, 0), SIB)
+        conv1d(0, first0)
+        second0 = conv2(0, {3: four, 10: two_off})
+        ready(1)
+        arrange(1)
+        first1 = conv1(1)
+        pooled0 = conv2d(0, second0)
         margins(0, pooled0)
+        conv1d(1, first1)
+        second1 = conv2(1, {10: three_off})
         ready(2)
-        arrange2 = arrange(2)
-        conv1d(1, first1)
-        arranged(2, arrange2)
+        arrange(2)
         first2 = conv1(2)
-        second1 = conv2(1)
+        pooled1 = conv2d(1, second1)
+        margins(1, pooled1)
+        ready(3)
+        arrange(3)
+        first3 = conv1(3)
         conv1d(2, first2)
-        ready(3)
-        arrange3 = arrange(3)
-        pooled1 = conv2d(1, second1)
-        arranged(3, arrange3)
-        first3 = conv1(3)
-        margins(1, pooled1)
-        second2 = conv2(2)
+        second2 = conv2(2, part=slice(0, 6))
         conv1d(3, first3)
-        pooled2 = conv2d(2, second2)
         second3 = conv2(3)
-        margins(2, pooled2)
-        margins(3, conv2d(3, second3))
+
+        def far():
+            margins(3, conv2d(3, second3))
+            tell(3)
+
+        conv2(2, {5: far}, second2, slice(6, None))
+        margins(2, conv2d(2, second2))
+        for g in (2, 1, 0):
+            tell(g)
 
         assert len(sent) == SENDS
         pltpu.make_async_copy(gathered.at[pl.ds(0, SENDS)], gathered.at[pl.ds(0, SENDS)], fsend).wait()
@@ -384,7 +381,7 @@
             pltpu.VMEM(conv1_weight.shape[1:], conv1_weight.dtype),
             pltpu.VMEM(conv2_weight.shape[1:], conv2_weight.dtype),
             pltpu.VMEM(head.shape, head.dtype),
-            pltpu.VMEM((n * spots, chans), jnp.float32),
+            pltpu.VMEM((chans // LANES, n * spots, LANES), jnp.float32),
             pltpu.VMEM((n * spots, chans), jnp.float32),
             pltpu.VMEM((n, LANES), jnp.float32),
             pltpu.SemaphoreType.REGULAR((2,)),

time: 33.6 us -> 31.1 us (0.926)
  Pallas kernels: 32.3 us -> 29.7 us
    pallas_call x1, Pallas kernels: 31.6 us -> 29 us  [shards(): pl.pallas_call(functools.partial(kernel, n), out_shape=pltpu.VMEM((n, LAN...]
where the time goes in v3:
time: 31.1 us; the launch traced here: 31 us
  Pallas kernels  29.7 us (95%)
  between operations  1.28 us (4%)
    pallas_call x1, Pallas kernels, shards(): pl.pallas_call(functools.partial(kernel, n), out_shape=pltpu.VMEM((n, LAN...  29 us
    pallas_call x1, Pallas kernels, shards(): pl.pallas_call(finish, out_shape=(jax.ShapeDtypeStruct((1, SUBSETS), jnp....  0.7 us

profile of v3, /device:TPU:1, one launch (start us, length us, event | category | flops | bytes accessed | tf_op | source)
XLA Modules:
  0.0 31.0 jit_solution(10622023912979108888)
XLA Ops:
  1.3 29.0 %shard_map.85.got = f32[64,128]{1,0:T(8,128)S(1)} custom-call(bf16[1,4,4,512]{3,2,1,0:T(4,128)(2,1)} %feat_ref.1, s32[64]{0:T(128)} %labels_ref.1, s32[1]{0:T(128)S(6)} %copy.9.ids_ref, bf16[1,9,512,512]{3,2,1,0:T(8,128)(2,1)} %w1_ref.1, bf16[1,9,512,512]{3,2,1,0:T(8,128)(2,1)} %w2_ref.1, f32[10,1,512]{2,1,0:T(1,128)} %bitcast.1), custom_call_target="tpu_custom_call" | custom-call | tf_op jit(solution)/shard_map/pallas_call | solution.py:372
  30.3 0.7 %shard_map.86 = (f32[1,256]{1,0:T(1,128)}, f32[1]{0:T(128)}, f32[1]{0:T(128)}) custom-call(f32[64,128]{1,0:T(8,128)S(1)} %shard_map.85.got), custom_call_target="tpu_custom_call" | custom-call | tf_op jit(solution)/shard_map/pallas_call | solution.py:403

commit v4 on v3

--- a/solution.py
+++ b/solution.py
@@ -175,9 +175,9 @@
             first = STARTS[g] * spots + p * t
             return (slice(first, first + t), slice(k * TILE, (k + 1) * TILE))
 
-        def arrange(g):
+        def arrange(g, span=(16,)):
             t = len(CHUNKS[g])
-            for i in range(t):
+            for i in range(*span):
                 for y in range(width):
                     first = STARTS[g] * spots + y * width * t + i
                     line = gathered[STARTS[g] + i, y].astype(jnp.float32)
@@ -230,7 +230,9 @@
 
         def tell(g):
             first = STARTS[g]
-            for i, r in enumerate(CHUNKS[g]):
+            hops = [abs(r[0]) + abs(r[1]) for r in CHUNKS[g]]
+            for i in sorted(range(len(hops)), key=lambda i: -hops[i]):
+                r = CHUNKS[g][i]
                 s = first + i
                 if r == (0, 0, 0):
                     got[0:1, :] = msg[0:1, :]
@@ -268,8 +270,9 @@
         pltpu.make_async_copy(w1, w1, w1_sem).wait()
         pltpu.make_async_copy(w2, w2, w2_sem).wait()
         head_copy.wait()
+        arrange(0, (0, 8))
         ready(0)
-        arrange(0)
+        arrange(0, (8, 16))
 
         def four():
             for z in BOTH:
@@ -297,14 +300,14 @@
             for z in BOTH:
                 pass_on((y, z, 0), SIB)
         conv1d(0, first0)
-        second0 = conv2(0, {3: four, 10: two_off})
+        second0 = conv2(0, {5: four, 16: two_off})
         ready(1)
         arrange(1)
         first1 = conv1(1)
         pooled0 = conv2d(0, second0)
         margins(0, pooled0)
         conv1d(1, first1)
-        second1 = conv2(1, {10: three_off})
+        second1 = conv2(1, {15: three_off})
         ready(2)
         arrange(2)
         first2 = conv1(2)
@@ -314,7 +317,7 @@
         arrange(3)
         first3 = conv1(3)
         conv1d(2, first2)
-        second2 = conv2(2, part=slice(0, 6))
+        second2 = conv2(2, part=slice(0, 3))
         conv1d(3, first3)
         second3 = conv2(3)
 
@@ -322,7 +325,7 @@
             margins(3, conv2d(3, second3))
             tell(3)
 
-        conv2(2, {5: far}, second2, slice(6, None))
+        conv2(2, {3: far}, second2, slice(3, None))
         margins(2, conv2d(2, second2))
         for g in (2, 1, 0):
             tell(g)

time: 31.1 us -> 30.9 us (level)
  no operation moved by 1% of the time
where the time goes in v4:
time: 30.9 us; the launch traced here: 30.8 us
  Pallas kernels  29.6 us (96%)
  between operations  1.28 us (4%)
    pallas_call x1, Pallas kernels, shards(): pl.pallas_call(functools.partial(kernel, n), out_shape=pltpu.VMEM((n, LAN...  28.9 us
    pallas_call x1, Pallas kernels, shards(): pl.pallas_call(finish, out_shape=(jax.ShapeDtypeStruct((1, SUBSETS), jnp....  0.7 us

profile of v4, /device:TPU:1, one launch (start us, length us, event | category | flops | bytes accessed | tf_op | source)
XLA Modules:
  0.0 30.8 jit_solution(16594062779130080369)
XLA Ops:
  1.3 28.9 %shard_map.85.got = f32[64,128]{1,0:T(8,128)S(1)} custom-call(bf16[1,4,4,512]{3,2,1,0:T(4,128)(2,1)} %feat_ref.1, s32[64]{0:T(128)} %labels_ref.1, s32[1]{0:T(128)S(6)} %copy.9.ids_ref, bf16[1,9,512,512]{3,2,1,0:T(8,128)(2,1)} %w1_ref.1, bf16[1,9,512,512]{3,2,1,0:T(8,128)(2,1)} %w2_ref.1, f32[10,1,512]{2,1,0:T(1,128)} %bitcast.1), custom_call_target="tpu_custom_call" | custom-call | tf_op jit(solution)/shard_map/pallas_call | solution.py:375
  30.1 0.7 %shard_map.86 = (f32[1,256]{1,0:T(1,128)}, f32[1]{0:T(128)}, f32[1]{0:T(128)}) custom-call(f32[64,128]{1,0:T(8,128)S(1)} %shard_map.85.got), custom_call_target="tpu_custom_call" | custom-call | tf_op jit(solution)/shard_map/pallas_call | solution.py:406

commit v5 on v4

--- a/solution.py
+++ b/solution.py
@@ -294,20 +294,20 @@
                 pass_on((2, 3 * z, 0), SIB)
 
         first0 = conv1(0)
-        for z in BOTH:
-            pass_on((0, 3 * z, 0), *COLUMN, SIB)
         for y in BOTH:
             for z in BOTH:
                 pass_on((y, z, 0), SIB)
+        for z in BOTH:
+            pass_on((0, 3 * z, 0), *COLUMN, SIB)
         conv1d(0, first0)
-        second0 = conv2(0, {5: four, 16: two_off})
+        second0 = conv2(0, {4: four})
         ready(1)
         arrange(1)
-        first1 = conv1(1)
+        first1 = conv1(1, {1: two_off})
         pooled0 = conv2d(0, second0)
         margins(0, pooled0)
         conv1d(1, first1)
-        second1 = conv2(1, {15: three_off})
+        second1 = conv2(1, {14: three_off})
         ready(2)
         arrange(2)
         first2 = conv1(2)

time: 30.9 us -> 31.5 us (1.019)
  Pallas kernels: 29.6 us -> 30.2 us
    pallas_call x1, Pallas kernels: 28.9 us -> 29.5 us  [shards(): pl.pallas_call(functools.partial(kernel, n), out_shape=pltpu.VMEM((n, LAN...]
where the time goes in v5:
time: 31.5 us; the launch traced here: 31.4 us
  Pallas kernels  30.2 us (96%)
  between operations  1.28 us (4%)
    pallas_call x1, Pallas kernels, shards(): pl.pallas_call(functools.partial(kernel, n), out_shape=pltpu.VMEM((n, LAN...  29.5 us
    pallas_call x1, Pallas kernels, shards(): pl.pallas_call(finish, out_shape=(jax.ShapeDtypeStruct((1, SUBSETS), jnp....  0.7 us

profile of v5, /device:TPU:1, one launch (start us, length us, event | category | flops | bytes accessed | tf_op | source)
XLA Modules:
  0.0 31.4 jit_solution(12853978415760599459)
XLA Ops:
  1.3 29.5 %shard_map.85.got = f32[64,128]{1,0:T(8,128)S(1)} custom-call(bf16[1,4,4,512]{3,2,1,0:T(4,128)(2,1)} %feat_ref.1, s32[64]{0:T(128)} %labels_ref.1, s32[1]{0:T(128)S(6)} %copy.9.ids_ref, bf16[1,9,512,512]{3,2,1,0:T(8,128)(2,1)} %w1_ref.1, bf16[1,9,512,512]{3,2,1,0:T(8,128)(2,1)} %w2_ref.1, f32[10,1,512]{2,1,0:T(1,128)} %bitcast.1), custom_call_target="tpu_custom_call" | custom-call | tf_op jit(solution)/shard_map/pallas_call | solution.py:375
  30.7 0.7 %shard_map.86 = (f32[1,256]{1,0:T(1,128)}, f32[1]{0:T(128)}, f32[1]{0:T(128)}) custom-call(f32[64,128]{1,0:T(8,128)S(1)} %shard_map.85.got), custom_call_target="tpu_custom_call" | custom-call | tf_op jit(solution)/shard_map/pallas_call | solution.py:406
